TPU v7x, 32 devices: a whole 2x2x4 slice. The times are simulated.
32 devices in a mesh: batch: 8 (over y, x, core), head: 4 (over z).
Axes of the slice: x: 2, y: 2, z: 4, core: 2. Of those that a mesh axis runs over, the one named last changes fastest.
Arguments:
- inputs: bfloat16 [8, 128, 2048], P(None, 'batch', 'head'), parts along dimension 1, may hold values from -6 to 6
- in_weight: bfloat16 [2048, 4, 384], P(None, 'head'), may hold values from -0.125 to 0.125
- gate_weight: bfloat16 [2048, 4], P(None, 'head'), may hold values from -0.125 to 0.125
- gate_bias: float32 [4], P('head'), may hold values from -2 to 3
- norm_gain: float32 [512], P('head'), may hold values from 0.1 to 1.9
- out_weight: bfloat16 [512, 2048], P('head'), may hold values from -0.375 to 0.375
- inv_gram: float32 [128, 4, 128, 128], P('batch', 'head'), parts along dimension 0, may hold values from -17 to 17, as said below
- value_key: float32 [128, 4, 128, 128], P('batch', 'head'), parts along dimension 0, may hold values from -6 to 6
Outputs:
- layer_out: float32 [8, 128, 2048], P(None, 'batch', 'head'), parts along dimension 1
There are 8 independent parts, one for each index of `batch`. A program takes and returns all parts, laid end to end along the dimension named above; an argument that names none is the same for every part. Nothing has to cross between parts.
Inputs may be any that keep to these rules, and one draw needn't show every extreme that they name: `inv_gram`: each [128, 128] matrix is symmetric positive definite.
All inputs are finite; a program needn't handle non-finite values.
Results may differ from a plain program's by a relative error of at most 0.0029.
Values may be sent and summed in bfloat16 or wider, within the bound.
No kernel may reach another device: no remote copies, remote signals or barrier semaphores. Data moves between devices by JAX's collectives and lax.ppermute only.
A program may use at most 64 MiB of HBM per device.

v0:
```python
import jax
import jax.numpy as jnp
from jax import lax
from jax.sharding import PartitionSpec as P


def advance(gram_inv, memory, projected, gate, gate_bias, head_size):
    batch_rows, local_heads = gate.shape
    pieces = projected.reshape(batch_rows, local_heads, 3 * head_size)
    queries = pieces[..., :head_size]
    keys_now = pieces[..., head_size : 2 * head_size]
    values_now = pieces[..., 2 * head_size :]
    forget = 0.8 + 0.2 * jax.nn.sigmoid(gate + gate_bias)
    keys_now = keys_now * lax.rsqrt(jnp.sum(keys_now * keys_now, axis=-1, keepdims=True) + 1e-06)
    queries = queries * lax.rsqrt(jnp.sum(queries * queries, axis=-1, keepdims=True) + 1e-06)
    gram_key = jnp.einsum("bhij,bhj->bhi", gram_inv, keys_now, precision=lax.Precision.HIGHEST)
    denominator = forget + jnp.sum(keys_now * gram_key, axis=-1)
    gram_inv = (
        gram_inv - gram_key[..., :, None] * gram_key[..., None, :] / denominator[..., None, None]
    ) / forget[..., None, None]
    memory = forget[..., None, None] * memory + values_now[..., :, None] * keys_now[..., None, :]
    gram_query = jnp.einsum("bhij,bhj->bhi", gram_inv, queries, precision=lax.Precision.HIGHEST)
    readout = jnp.einsum("bhij,bhj->bhi", memory, gram_query, precision=lax.Precision.HIGHEST)
    return (gram_inv, memory, readout.reshape(batch_rows, local_heads * head_size))


def local(inputs, in_weight, gate_weight, gate_bias, norm_gain, out_weight, inv_gram, value_key):
    step_count, batch_rows, _ = inputs.shape
    d_model = in_weight.shape[0]
    local_heads = in_weight.shape[1]
    head_size = in_weight.shape[2] // 3
    total_width = local_heads * head_size * lax.axis_size("head")
    weight_flat = in_weight.reshape(d_model, local_heads * 3 * head_size)
    gram_inv = inv_gram
    memory = value_key
    readouts = []
    for position in range(step_count):
        rows = lax.all_gather(inputs[position], "head", axis=1, tiled=True)
        projected = jnp.dot(rows, weight_flat, preferred_element_type=jnp.float32)
        gate = jnp.dot(rows, gate_weight, preferred_element_type=jnp.float32)
        gram_inv, memory, readout = advance(gram_inv, memory, projected, gate, gate_bias, head_size)
        readouts.append(readout)
    readout_all = jnp.stack(readouts, axis=0)
    squares = lax.psum(jnp.sum(readout_all * readout_all, axis=-1), "head")
    hidden = (
        norm_gain * readout_all * lax.rsqrt(squares / total_width + 1e-06)[:, :, None]
    ).astype(jnp.bfloat16)
    partial_out = jnp.dot(
        hidden.reshape(step_count * batch_rows, -1), out_weight, preferred_element_type=jnp.float32
    )
    partial_out = partial_out.reshape(step_count, batch_rows, d_model)
    return lax.psum_scatter(partial_out, "head", scatter_dimension=2, tiled=True)


def solution(mesh):
    in_specs = (
        P(None, "batch", "head"),
        P(None, "head", None),
        P(None, "head"),
        P("head"),
        P("head"),
        P("head", None),
        P("batch", "head", None, None),
        P("batch", "head", None, None),
    )
    out_specs = P(None, "batch", "head")
    return jax.shard_map(local, mesh=mesh, in_specs=in_specs, out_specs=out_specs, check_vma=False)
```

profile of v0, /device:TPU:0, one launch (start us, length us, event | category | flops | bytes accessed | tf_op | source)
XLA Modules:
  0.0 223.0 jit_solution(10314637504935739932)
XLA Ops:
  7.5 14.9 %all-gather = bf16[1,16,2048]{2,1,0:T(8,128)(2,1)S(1)} all-gather(bf16[1,16,512]{2,1,0:T(8,128)(2,1)S(1)} %get-tuple-element.27), channel_id=2, replica_groups=mesh['batch'=8,'head'=4] {'head'}, dimensions={2}, use_global_device_ids=true | all-gather | bytes 81920 | tf_op jit(solution)/shard_map/all_gather | solution.py:38
  23.0 1.7 fusion.132
  27.8 1.9 fusion.134
  29.7 13.3 %all-gather.1 = bf16[1,16,2048]{2,1,0:T(8,128)(2,1)S(1)} all-gather(bf16[1,16,512]{2,1,0:T(8,128)(2,1)S(1)} %get-tuple-element.26), channel_id=3, replica_groups=mesh['batch'=8,'head'=4] {'head'}, dimensions={2}, use_global_device_ids=true | all-gather | bytes 81920 | tf_op jit(solution)/shard_map/all_gather | solution.py:38
  43.4 13.2 %all-gather.3 = bf16[1,16,2048]{2,1,0:T(8,128)(2,1)S(1)} all-gather(bf16[1,16,512]{2,1,0:T(8,128)(2,1)S(1)} %get-tuple-element.24), channel_id=5, replica_groups=mesh['batch'=8,'head'=4] {'head'}, dimensions={2}, use_global_device_ids=true | all-gather | bytes 81920 | tf_op jit(solution)/shard_map/all_gather | solution.py:38
  57.2 13.4 %all-gather.2 = bf16[1,16,2048]{2,1,0:T(8,128)(2,1)S(1)} all-gather(bf16[1,16,512]{2,1,0:T(8,128)(2,1)S(1)} %get-tuple-element.25), channel_id=4, replica_groups=mesh['batch'=8,'head'=4] {'head'}, dimensions={2}, use_global_device_ids=true | all-gather | bytes 81920 | tf_op jit(solution)/shard_map/all_gather | solution.py:38
  73.4 2.2 multiply_add_fusion.3
  77.4 2.1 fusion.127
  79.5 1.7 fusion.124
  83.5 2.6 %fusion.122 = f32[16,1,128]{2,1,0:T(1,128)S(1)} fusion(f32[16,128,1]{1,2,0:T(1,128)S(1)} %convolution_bitcast_fusion.5, f32[16,128]{1,0:T(8,128)S(1)} %bitcast.573, f32[16,128]{1,0:T(8,128)S(1)} %get-tuple-element.44, f32[16]{0:T(128)S(1)} %fusion.81, f32[16,1,128,128]{3,2,1,0:T(8,128)S(1)} %copy-done.2, f32[16,128]{1,0:T(8,128)S(1)} %bitcast.568, ...), kind=kOutput, calls=%fused_computation.122 | convolution fusion | flops 5505024 | bytes 1114304 | tf_op jit(solution)/shard_map/bhij,bhj->bhi/dot_general | solution.py:23
  86.1 1.7 fusion.119
  88.0 13.5 %all-gather.4 = bf16[1,16,2048]{2,1,0:T(8,128)(2,1)S(1)} all-gather(bf16[1,16,512]{2,1,0:T(8,128)(2,1)S(1)} %get-tuple-element.23), channel_id=6, replica_groups=mesh['batch'=8,'head'=4] {'head'}, dimensions={2}, use_global_device_ids=true | all-gather | bytes 81920 | tf_op jit(solution)/shard_map/all_gather | solution.py:38
  106.4 13.1 %all-gather.5 = bf16[1,16,2048]{2,1,0:T(8,128)(2,1)S(1)} all-gather(bf16[1,16,512]{2,1,0:T(8,128)(2,1)S(1)} %get-tuple-element.22), channel_id=7, replica_groups=mesh['batch'=8,'head'=4] {'head'}, dimensions={2}, use_global_device_ids=true | all-gather | bytes 81920 | tf_op jit(solution)/shard_map/all_gather | solution.py:38
  125.0 13.1 %all-gather.6 = bf16[1,16,2048]{2,1,0:T(8,128)(2,1)S(1)} all-gather(bf16[1,16,512]{2,1,0:T(8,128)(2,1)S(1)} %get-tuple-element.28), channel_id=8, replica_groups=mesh['batch'=8,'head'=4] {'head'}, dimensions={2}, use_global_device_ids=true | all-gather | bytes 81920 | tf_op jit(solution)/shard_map/all_gather | solution.py:38
  144.1 13.5 %all-gather.7 = bf16[1,16,2048]{2,1,0:T(8,128)(2,1)S(1)} all-gather(bf16[1,16,512]{2,1,0:T(8,128)(2,1)S(1)} %get-tuple-element.21), channel_id=9, replica_groups=mesh['batch'=8,'head'=4] {'head'}, dimensions={2}, use_global_device_ids=true | all-gather | bytes 81920 | tf_op jit(solution)/shard_map/all_gather | solution.py:38
  158.1 2.0 subtract_divide_fusion
  161.9 1.7 fusion.99
  165.5 1.9 fusion.112
  167.4 2.1 fusion.107
  169.5 2.6 %fusion.102 = f32[16,1,128]{2,1,0:T(1,128)S(1)} fusion(f32[16,128,1]{1,2,0:T(1,128)S(1)} %convolution_bitcast_fusion.1, f32[16,128]{1,0:T(8,128)S(1)} %bitcast.579, f32[16,128]{1,0:T(8,128)S(1)} %get-tuple-element.32, f32[16]{0:T(128)S(1)} %get-tuple-element.64, f32[16,1,128,128]{3,2,1,0:T(8,128)S(1)} %get-tuple-element.53, f32[16,128]{1,0:T(8,128)S(1)} %bitcast.576, ...), kind=kOutput, calls=%fused_computation.102 | convolution fusion | flops 5505024 | bytes 1114304 | tf_op jit(solution)/shard_map/bhij,bhj->bhi/dot_general | solution.py:23
  172.3 1.9 convolution_bitcast_fusion
  174.2 3.3 %fusion.97 = f32[16,1,128]{2,1,0:T(1,128)S(1)} fusion(f32[16,128,1]{1,2,0:T(1,128)S(1)} %convolution_bitcast_fusion, f32[16,128]{1,0:T(8,128)S(1)} %bitcast.582, f32[16,128]{1,0:T(8,128)S(1)} %get-tuple-element.29, f32[16]{0:T(128)S(1)} %get-tuple-element.66, f32[16,128]{1,0:T(8,128)S(1)} %bitcast.580, f32[16,128]{1,0:T(8,128)S(1)} %get-tuple-element.32, ...), kind=kOutput, calls=%fused_computation.97 | convolution fusion | flops 6291456 | bytes 1130752 | tf_op jit(solution)/shard_map/bhij,bhj->bhi/dot_general | solution.py:23
  177.6 11.6 %psum.7 = f32[8,16]{1,0:T(8,128)S(1)} all-reduce(f32[8,16]{1,0:T(8,128)S(1)} %multiply_reduce_fusion), channel_id=1, replica_groups=mesh['batch'=8,'head'=4] {'head'}, use_global_device_ids=true, to_apply=%region_25.0 | all-reduce | flops 128 | bytes 1024 | tf_op jit(solution)/shard_map/psum | solution.py:44
  190.5 25.6 %reduce-scatter.2.cloned.1.call-done = f32[8,16,512]{2,1,0:T(8,128)} async-done(((f32[8,16,2048]{2,1,0:T(8,128)}), f32[8,16,512]{2,1,0:T(8,128)}) %reduce-scatter.2.cloned.1.call-update) | async-done | bytes 262160 | tf_op jit(solution)/shard_map/reduce_scatter | solution.py:52
  (93 shorter events, 33.9 us)
Async XLA Ops:
  6.5 15.9 %copy-start = (bf16[2048,1,384]{2,0,1:T(8,128)(2,1)S(1)}, bf16[2048,1,384]{2,0,1:T(8,128)(2,1)}, u32[]{:S(2)}) copy-start(bf16[2048,1,384]{2,0,1:T(8,128)(2,1)} %param.9) | copy-start | bytes 4718596
  6.5 16.4 %copy-start.1 = (f32[16,1,128,128]{3,2,1,0:T(8,128)S(1)}, f32[16,1,128,128]{3,2,1,0:T(8,128)}, u32[]{:S(2)}) copy-start(f32[16,1,128,128]{3,2,1,0:T(8,128)} %param.14) | copy-start | bytes 3145732
  6.5 19.0 %copy-start.5 = (bf16[2048,1]{0,1:T(2,128)(2,1)S(1)}, bf16[2048,1]{0,1:T(2,128)(2,1)}, u32[]{:S(2)}) copy-start(bf16[2048,1]{0,1:T(2,128)(2,1)} %param.10) | copy-start | bytes 12292
  6.5 209.6 %reduce-scatter.2.cloned.1.call-start = ((), (), s32[]{:S(2)}) async-start(), calls=%async_computation.1 | async-start | bytes 1310720 | tf_op jit(solution)/shard_map/reduce_scatter | solution.py:52
  25.7 2.1 copy-start.2
  174.2 15.0 %copy-start.3 = (bf16[128,2048]{1,0:T(8,128)(2,1)S(1)}, bf16[128,2048]{1,0:T(8,128)(2,1)}, u32[]{:S(2)}) copy-start(bf16[128,2048]{1,0:T(8,128)(2,1)} %param.13) | copy-start | bytes 1572868
  174.2 15.0 %copy-start.4 = (f32[128]{0:T(128)S(1)}, f32[128]{0:T(128)}, u32[]{:S(2)}) copy-start(f32[128]{0:T(128)} %param.12) | copy-start | bytes 1540
Sparse Core Ops, SparseCore 0:
  190.6 25.4 reduce-scatter.1
where the time goes:
time: 223 us
  blocking collectives  120 us (54%)
  matrix products  50.9 us (23%)
  waiting for transfers between devices  25.7 us (12%)
  between operations  14.4 us (6%)
  other arithmetic  11.4 us (5%)
    all_gather x8, blocking collectives, local(): rows = lax.all_gather(inputs[position], 'head', axis=1, tiled=True)  108 us
    reduce_scatter x1, waiting for transfers between devices, local(): lax.psum_scatter(partial_out, 'head', scatter_dimension=2, tiled=True)  25.6 us
    dot_general x8, matrix products, advance(): jnp.einsum('bhij,bhj->bhi', memory, gram_query, precision=lax.Precision.H...  18.2 us
    dot_general x8, matrix products, advance(): jnp.einsum('bhij,bhj->bhi', gram_inv, queries, precision=lax.Precision.HI...  13.9 us
    dot_general x8, matrix products, advance(): jnp.einsum('bhij,bhj->bhi', gram_inv, keys_now, precision=lax.Precision.H...  13.9 us
    psum x1, blocking collectives, local(): squares = lax.psum(jnp.sum(readout_all * readout_all, axis=-1), 'head')  11.6 us
    div x6, other arithmetic, advance(): (gram_inv - gram_key[..., :, None] * gram_key[..., None, :] / denominator...  6.41 us
  transfers between devices with their start and end apart: 1, of which 1 were waited for; matrix products, arithmetic and copies ran while one was open for 0% of the time, Pallas kernels for 0%

commit v1 on v0

--- a/solution.py
+++ b/solution.py
@@ -35,7 +35,13 @@
     memory = value_key
     readouts = []
     for position in range(step_count):
-        rows = lax.all_gather(inputs[position], "head", axis=1, tiled=True)
+        x = inputs[position]
+        ways, here, step = (lax.axis_size("head"), lax.axis_index("head"), x.shape[1])
+        lengths = [n * ways if d == 1 else n for d, n in enumerate(x.shape)]
+        rows = lax.dynamic_update_slice_in_dim(jnp.zeros(lengths, x.dtype), x, here * step, axis=1)
+        for far in range(1, ways):
+            x = lax.ppermute(x, "head", [(d, (d + 1) % ways) for d in range(ways)])
+            rows = lax.dynamic_update_slice_in_dim(rows, x, (here - far) % ways * step, axis=1)
         projected = jnp.dot(rows, weight_flat, preferred_element_type=jnp.float32)
         gate = jnp.dot(rows, gate_weight, preferred_element_type=jnp.float32)
         gram_inv, memory, readout = advance(gram_inv, memory, projected, gate, gate_bias, head_size)

time: 223 us -> 155 us (0.70)
  blocking collectives: 120 us -> 11.6 us
  starting transfers between devices: 0.01 us -> 31.2 us
  local copies, waits for them, and re-layouts: 1.04 us -> 7.18 us
    all_gather x8 -> x0, blocking collectives: 108 us -> none  [local(): rows = lax.all_gather(inputs[position], 'head', axis=1, tiled=True)]
    ppermute x0 -> x24, starting transfers between devices: none -> 31.2 us  [local(): x = lax.ppermute(x, 'head', [(d, (d + 1) % ways) for d in range(ways)])]
    dynamic_update_slice x0 -> x29, local copies, waits for them, and re-layouts: none -> 5.89 us  [the longest x8 5.81 us: local(): lax.dynamic_update_slice_in_dim(jnp.zeros(lengths, x.dtype), x, here * st...]
  transfers between devices with their start and end apart: 1 -> 25, of which waited for: 1 -> 2; matrix products, arithmetic and copies ran while one was open for 0% -> 27% of each run, Pallas kernels for 0% -> 0%
where the time goes in v1:
time: 155 us; the launch traced here: 154 us
  matrix products  51.2 us (33%)
  starting transfers between devices  31.2 us (20%)
  waiting for transfers between devices  26.2 us (17%)
  between operations  14.6 us (9%)
  other arithmetic  11.7 us (8%)
  blocking collectives  11.6 us (7%)
  local copies, waits for them, and re-layouts  7.18 us (5%)
    ppermute x24, starting transfers between devices, local(): x = lax.ppermute(x, 'head', [(d, (d + 1) % ways) for d in range(ways)])  31.2 us
    reduce_scatter x1, waiting for transfers between devices, local(): lax.psum_scatter(partial_out, 'head', scatter_dimension=2, tiled=True)  25.6 us
    dot_general x8, matrix products, advance(): jnp.einsum('bhij,bhj->bhi', memory, gram_query, precision=lax.Precision.H...  18.4 us
    dot_general x8, matrix products, advance(): jnp.einsum('bhij,bhj->bhi', gram_inv, queries, precision=lax.Precision.HI...  13.9 us
    dot_general x8, matrix products, advance(): jnp.einsum('bhij,bhj->bhi', gram_inv, keys_now, precision=lax.Precision.H...  13.9 us
    psum x1, blocking collectives, local(): squares = lax.psum(jnp.sum(readout_all * readout_all, axis=-1), 'head')  11.6 us
    div x6, other arithmetic, advance(): (gram_inv - gram_key[..., :, None] * gram_key[..., None, :] / denominator...  6.64 us
    dynamic_update_slice x8, local copies, waits for them, and re-layouts, local(): lax.dynamic_update_slice_in_dim(jnp.zeros(lengths, x.dtype), x, here * st...  5.81 us
  transfers between devices with their start and end apart: 25, of which 2 were waited for; matrix products, arithmetic and copies ran while one was open for 27% of the time, Pallas kernels for 0%

profile of v1, /device:TPU:0, one launch (start us, length us, event | category | flops | bytes accessed | tf_op | source)
XLA Modules:
  0.0 153.7 jit_solution(891321028439918103)
XLA Ops:
  7.5 3.1 %collective-permute-start.3 = (bf16[16,512]{1,0:T(8,128)(2,1)S(1)}, bf16[16,512]{1,0:T(8,128)(2,1)S(1)}, u32[]{:S(2)}, u32[]{:S(2)}) collective-permute-start(bf16[16,512]{1,0:T(8,128)(2,1)S(1)} %get-tuple-element.26), channel_id=1, source_target_pairs={{0,1},{1,2},{2,3},{3,0},{4,5},{5,6},{6,7},{7,4},{8,9},{9,10},{10,1... | collective-permute-start | bytes 49160 | tf_op jit(solution)/shard_map/ppermute | solution.py:43
  13.8 1.7 %collective-permute-start.15 = (bf16[16,512]{1,0:T(8,128)(2,1)S(1)}, bf16[16,512]{1,0:T(8,128)(2,1)S(1)}, u32[]{:S(2)}, u32[]{:S(2)}) collective-permute-start(bf16[16,512]{1,0:T(8,128)(2,1)S(1)} %get-tuple-element.22), channel_id=1, source_target_pairs={{0,1},{1,2},{2,3},{3,0},{4,5},{5,6},{6,7},{7,4},{8,9},{9,10},{10,1... | collective-permute-start | bytes 49160 | tf_op jit(solution)/shard_map/ppermute | solution.py:43
  46.5 1.7 %fusion.132 = f32[16,1,128]{2,1,0:T(1,128)S(1)} fusion(f32[16,128,1]{1,2,0:T(1,128)S(1)} %bitcast.547, f32[16,1,128,128]{3,2,1,0:T(8,128)S(1)} %copy-done.1), kind=kOutput, calls=%fused_computation.132 | convolution fusion | flops 3145728 | bytes 1064960 | tf_op jit(solution)/shard_map/bhij,bhj->bhi/dot_general | solution.py:16
  52.5 1.7 %fusion.129 = f32[16,1,128]{2,1,0:T(1,128)S(1)} fusion(f32[16,128,1]{1,2,0:T(1,128)S(1)} %bitcast.561, f32[16,1,128,128]{3,2,1,0:T(8,128)S(1)} %subtract_divide_fusion.6), kind=kOutput, calls=%fused_computation.129 | convolution fusion | flops 3145728 | bytes 1064960 | tf_op jit(solution)/shard_map/bhij,bhj->bhi/dot_general | solution.py:16
  54.7 1.8 %fusion.134 = f32[16,1,128]{2,1,0:T(1,128)S(1)} fusion(f32[16,128,1]{1,2,0:T(1,128)S(1)} %convolution_bitcast_fusion.7, f32[16,1,128,128]{3,2,1,0:T(8,128)S(1)} %copy-done.2, f32[16,128]{1,0:T(8,128)S(1)} %bitcast.548, f32[16,128]{1,0:T(8,128)S(1)} %get-tuple-element.50, f32[16]{0:T(128)S(1)} %get-tuple-element.56), kind=kOutput, calls=%fused_computation.134 | convolution fusion | flops 3932160 | bytes 1081408 | tf_op jit(solution)/shard_map/bhij,bhj->bhi/dot_general | solution.py:23
  56.6 2.4 %multiply_add_fusion.3 = (f32[16,1,128,128]{3,2,1,0:T(8,128)S(1)}, f32[16,1,128,128]{3,2,1,0:T(8,128)S(1)}) fusion(f32[16,128]{1,0:T(8,128)S(1)} %bitcast.565, f32[16,128]{1,0:T(8,128)S(1)} %get-tuple-element.41, f32[16]{0:T(128)S(1)} %fusion.74, f32[16,128]{1,0:T(8,128)S(1)} %bitcast.567, f32[16,128]{1,0:T(8,128)S(1)} %get-tuple-element.44, ...), kind=kLoop, calls=%fused_computation.150 | loop fusion | flops 5242880 | bytes 4276608 | tf_op jit(solution)/shard_map/add | solution.py:21
  60.6 2.1 %fusion.127 = f32[16,1,128]{2,1,0:T(1,128)S(1)} fusion(f32[16,128,1]{1,2,0:T(1,128)S(1)} %convolution_bitcast_fusion.6, f32[16,1,128,128]{3,2,1,0:T(8,128)S(1)} %copy-done.2, f32[16,128]{1,0:T(8,128)S(1)} %bitcast.563, f32[16,128]{1,0:T(8,128)S(1)} %get-tuple-element.47, f32[16]{0:T(128)S(1)} %get-tuple-element.58, f32[16,128]{1,0:T(8,128)S(1)} %bitcast.550, ...), kind=kOutput, calls=%fused_computation.127 | convolution fusion | flops 4718592 | bytes 1097856 | tf_op jit(solution)/shard_map/bhij,bhj->bhi/dot_general | solution.py:23
  62.8 1.7 %fusion.124 = f32[16,1,128]{2,1,0:T(1,128)S(1)} fusion(f32[16,128,1]{1,2,0:T(1,128)S(1)} %bitcast.568, f32[16,1,128,128]{3,2,1,0:T(8,128)S(1)} %get-tuple-element.54), kind=kOutput, calls=%fused_computation.124 | convolution fusion | flops 3145728 | bytes 1064960 | tf_op jit(solution)/shard_map/bhij,bhj->bhi/dot_general | solution.py:16
  65.0 1.7 %convolution_bitcast_fusion.5 = f32[16,128,1]{1,2,0:T(1,128)S(1)} fusion(f32[16,128,1]{1,2,0:T(1,128)S(1)} %bitcast.584, f32[16,1,128,128]{3,2,1,0:T(8,128)S(1)} %subtract_divide_fusion.4), kind=kOutput, calls=%fused_computation.29 | convolution fusion | flops 3145728 | bytes 1064960 | tf_op jit(solution)/shard_map/bhij,bhj->bhi/dot_general | solution.py:22
  66.8 2.6 %fusion.122 = f32[16,1,128]{2,1,0:T(1,128)S(1)} fusion(f32[16,128,1]{1,2,0:T(1,128)S(1)} %convolution_bitcast_fusion.5, f32[16,128]{1,0:T(8,128)S(1)} %bitcast.569, f32[16,128]{1,0:T(8,128)S(1)} %get-tuple-element.44, f32[16]{0:T(128)S(1)} %fusion.81, f32[16,1,128,128]{3,2,1,0:T(8,128)S(1)} %copy-done.2, f32[16,128]{1,0:T(8,128)S(1)} %bitcast.564, ...), kind=kOutput, calls=%fused_computation.122 | convolution fusion | flops 5505024 | bytes 1114304 | tf_op jit(solution)/shard_map/bhij,bhj->bhi/dot_general | solution.py:23
  69.4 1.7 %fusion.119 = f32[16,1,128]{2,1,0:T(1,128)S(1)} fusion(f32[16,128,1]{1,2,0:T(1,128)S(1)} %bitcast.566, f32[16,1,128,128]{3,2,1,0:T(8,128)S(1)} %subtract_divide_fusion.4), kind=kOutput, calls=%fused_computation.119 | convolution fusion | flops 3145728 | bytes 1064960 | tf_op jit(solution)/shard_map/bhij,bhj->bhi/dot_general | solution.py:16
  74.3 1.7 %fusion.114 = f32[16,1,128]{2,1,0:T(1,128)S(1)} fusion(f32[16,128,1]{1,2,0:T(1,128)S(1)} %bitcast.556, f32[16,1,128,128]{3,2,1,0:T(8,128)S(1)} %subtract_divide_fusion.3), kind=kOutput, calls=%fused_computation.114 | convolution fusion | flops 3145728 | bytes 1064960 | tf_op jit(solution)/shard_map/bhij,bhj->bhi/dot_general | solution.py:16
  80.1 1.7 %fusion.109 = f32[16,1,128]{2,1,0:T(1,128)S(1)} fusion(f32[16,128,1]{1,2,0:T(1,128)S(1)} %bitcast.570, f32[16,1,128,128]{3,2,1,0:T(8,128)S(1)} %subtract_divide_fusion.2), kind=kOutput, calls=%fused_computation.109 | convolution fusion | flops 3145728 | bytes 1064960 | tf_op jit(solution)/shard_map/bhij,bhj->bhi/dot_general | solution.py:16
  86.0 1.7 %fusion.104 = f32[16,1,128]{2,1,0:T(1,128)S(1)} fusion(f32[16,128,1]{1,2,0:T(1,128)S(1)} %bitcast.574, f32[16,1,128,128]{3,2,1,0:T(8,128)S(1)} %subtract_divide_fusion.1), kind=kOutput, calls=%fused_computation.104 | convolution fusion | flops 3145728 | bytes 1064960 | tf_op jit(solution)/shard_map/bhij,bhj->bhi/dot_general | solution.py:16
  88.5 2.0 %subtract_divide_fusion = f32[16,1,128,128]{3,2,1,0:T(8,128)S(1)} fusion(f32[16]{0:T(128)S(1)} %get-tuple-element.63, f32[16,128]{1,0:T(8,128)S(1)} %bitcast.555, f32[16]{0:T(128)S(1)} %get-tuple-element.64, f32[16]{0:T(128)S(1)} %get-tuple-element.62, f32[16]{0:T(128)S(1)} %get-tuple-element.61, f32[16,128]{1,0:T(8,128)S(1)} %bitcast.546, ...), kind=kLoop, calls=%fused_computation.143 | loop fusion | flops 5242880 | bytes 2138752 | tf_op jit(solution)/shard_map/div | solution.py:18
  92.3 1.7 %fusion.99 = f32[16,1,128]{2,1,0:T(1,128)S(1)} fusion(f32[16,128,1]{1,2,0:T(1,128)S(1)} %bitcast.577, f32[16,1,128,128]{3,2,1,0:T(8,128)S(1)} %subtract_divide_fusion), kind=kOutput, calls=%fused_computation.99 | convolution fusion | flops 3145728 | bytes 1064960 | tf_op jit(solution)/shard_map/bhij,bhj->bhi/dot_general | solution.py:16
  94.2 1.7 %fusion.117 = f32[16,1,128]{2,1,0:T(1,128)S(1)} fusion(f32[16,128,1]{1,2,0:T(1,128)S(1)} %convolution_bitcast_fusion.4, f32[16,1,128,128]{3,2,1,0:T(8,128)S(1)} %get-tuple-element.53), kind=kOutput, calls=%fused_computation.117 | convolution fusion | flops 3145728 | bytes 1064960 | tf_op jit(solution)/shard_map/bhij,bhj->bhi/dot_general | solution.py:23
  95.9 1.9 %fusion.112 = f32[16,1,128]{2,1,0:T(1,128)S(1)} fusion(f32[16,128,1]{1,2,0:T(1,128)S(1)} %convolution_bitcast_fusion.3, f32[16,1,128,128]{3,2,1,0:T(8,128)S(1)} %get-tuple-element.53, f32[16,128]{1,0:T(8,128)S(1)} %bitcast.557, f32[16,128]{1,0:T(8,128)S(1)} %get-tuple-element.38, f32[16]{0:T(128)S(1)} %get-tuple-element.60), kind=kOutput, calls=%fused_computation.112 | convolution fusion | flops 3932160 | bytes 1081408 | tf_op jit(solution)/shard_map/bhij,bhj->bhi/dot_general | solution.py:23
  97.8 2.1 %fusion.107 = f32[16,1,128]{2,1,0:T(1,128)S(1)} fusion(f32[16,128,1]{1,2,0:T(1,128)S(1)} %convolution_bitcast_fusion.2, f32[16,1,128,128]{3,2,1,0:T(8,128)S(1)} %get-tuple-element.53, f32[16,128]{1,0:T(8,128)S(1)} %bitcast.571, f32[16,128]{1,0:T(8,128)S(1)} %get-tuple-element.35, f32[16]{0:T(128)S(1)} %get-tuple-element.62, f32[16,128]{1,0:T(8,128)S(1)} %bitcast.558, ...), kind=kOutput, calls=%fused_computation.107 | convolution fusion | flops 4718592 | bytes 1097856 | tf_op jit(solution)/shard_map/bhij,bhj->bhi/dot_general | solution.py:23
  99.9 2.8 %fusion.102 = f32[16,1,128]{2,1,0:T(1,128)S(1)} fusion(f32[16,128,1]{1,2,0:T(1,128)S(1)} %convolution_bitcast_fusion.1, f32[16,128]{1,0:T(8,128)S(1)} %bitcast.575, f32[16,128]{1,0:T(8,128)S(1)} %get-tuple-element.32, f32[16]{0:T(128)S(1)} %get-tuple-element.64, f32[16,1,128,128]{3,2,1,0:T(8,128)S(1)} %get-tuple-element.53, f32[16,128]{1,0:T(8,128)S(1)} %bitcast.572, ...), kind=kOutput, calls=%fused_computation.102 | convolution fusion | flops 5505024 | bytes 1114304 | tf_op jit(solution)/shard_map/bhij,bhj->bhi/dot_general | solution.py:23
  102.9 1.9 %convolution_bitcast_fusion = f32[16,128,1]{1,2,0:T(1,128)S(1)} fusion(f32[16,128,1]{1,2,0:T(1,128)S(1)} %bitcast.591, f32[16,1,128,128]{3,2,1,0:T(8,128)S(1)} %subtract_divide_fusion, f32[16]{0:T(128)S(1)} %get-tuple-element.65, f32[16,128]{1,0:T(8,128)S(1)} %bitcast.588, f32[16]{0:T(128)S(1)} %get-tuple-element.66), kind=kOutput, calls=%fused_computation.24 | convolution fusion | flops 4194304 | bytes 1073280 | tf_op jit(solution)/shard_map/bhij,bhj->bhi/dot_general | solution.py:22
  104.8 3.3 %fusion.97 = f32[16,1,128]{2,1,0:T(1,128)S(1)} fusion(f32[16,128,1]{1,2,0:T(1,128)S(1)} %convolution_bitcast_fusion, f32[16,128]{1,0:T(8,128)S(1)} %bitcast.578, f32[16,128]{1,0:T(8,128)S(1)} %get-tuple-element.29, f32[16]{0:T(128)S(1)} %get-tuple-element.66, f32[16,128]{1,0:T(8,128)S(1)} %bitcast.576, f32[16,128]{1,0:T(8,128)S(1)} %get-tuple-element.32, ...), kind=kOutput, calls=%fused_computation.97 | convolution fusion | flops 6291456 | bytes 1130752 | tf_op jit(solution)/shard_map/bhij,bhj->bhi/dot_general | solution.py:23
  108.2 11.6 %psum.7 = f32[8,16]{1,0:T(8,128)S(1)} all-reduce(f32[8,16]{1,0:T(8,128)S(1)} %multiply_reduce_fusion), channel_id=1, replica_groups=mesh['batch'=8,'head'=4] {'head'}, use_global_device_ids=true, to_apply=%region_25.26 | all-reduce | flops 128 | bytes 1024 | tf_op jit(solution)/shard_map/psum | solution.py:50
  121.2 25.6 %reduce-scatter.2.cloned.1.call-done = f32[8,16,512]{2,1,0:T(8,128)} async-done(((f32[8,16,2048]{2,1,0:T(8,128)}), f32[8,16,512]{2,1,0:T(8,128)}) %reduce-scatter.2.cloned.1.call-update) | async-done | bytes 262160 | tf_op jit(solution)/shard_map/reduce_scatter | solution.py:58
  (176 shorter events, 56.8 us)
Async XLA Ops:
  6.5 140.3 %reduce-scatter.2.cloned.1.call-start = ((), (), s32[]{:S(2)}) async-start(), calls=%async_computation.1 | async-start | bytes 1310720 | tf_op jit(solution)/shard_map/reduce_scatter | solution.py:58
  7.5 14.6 %collective-permute-start.3 = (bf16[16,512]{1,0:T(8,128)(2,1)S(1)}, bf16[16,512]{1,0:T(8,128)(2,1)S(1)}, u32[]{:S(2)}, u32[]{:S(2)}) collective-permute-start(bf16[16,512]{1,0:T(8,128)(2,1)S(1)} %get-tuple-element.26), channel_id=1, source_target_pairs={{0,1},{1,2},{2,3},{3,0},{4,5},{5,6},{6,7},{7,4},{8,9},{9,10},{10,1... | collective-permute-start | bytes 49160 | tf_op jit(solution)/shard_map/ppermute | solution.py:43
  10.6 13.1 %collective-permute-start = (bf16[16,512]{1,0:T(8,128)(2,1)S(1)}, bf16[16,512]{1,0:T(8,128)(2,1)S(1)}, u32[]{:S(2)}, u32[]{:S(2)}) collective-permute-start(bf16[16,512]{1,0:T(8,128)(2,1)S(1)} %get-tuple-element.27), channel_id=1, source_target_pairs={{0,1},{1,2},{2,3},{3,0},{4,5},{5,6},{6,7},{7,4},{8,9},{9,10},{10,1... | collective-permute-start | bytes 49160 | tf_op jit(solution)/shard_map/ppermute | solution.py:43
  12.2 13.2 %collective-permute-start.9 = (bf16[16,512]{1,0:T(8,128)(2,1)S(1)}, bf16[16,512]{1,0:T(8,128)(2,1)S(1)}, u32[]{:S(2)}, u32[]{:S(2)}) collective-permute-start(bf16[16,512]{1,0:T(8,128)(2,1)S(1)} %get-tuple-element.24), channel_id=1, source_target_pairs={{0,1},{1,2},{2,3},{3,0},{4,5},{5,6},{6,7},{7,4},{8,9},{9,10},{10,1... | collective-permute-start | bytes 49160 | tf_op jit(solution)/shard_map/ppermute | solution.py:43
  13.8 11.7 %collective-permute-start.6 = (bf16[16,512]{1,0:T(8,128)(2,1)S(1)}, bf16[16,512]{1,0:T(8,128)(2,1)S(1)}, u32[]{:S(2)}, u32[]{:S(2)}) collective-permute-start(bf16[16,512]{1,0:T(8,128)(2,1)S(1)} %get-tuple-element.25), channel_id=1, source_target_pairs={{0,1},{1,2},{2,3},{3,0},{4,5},{5,6},{6,7},{7,4},{8,9},{9,10},{10,1... | collective-permute-start | bytes 49160 | tf_op jit(solution)/shard_map/ppermute | solution.py:43
  13.8 13.3 %collective-permute-start.15 = (bf16[16,512]{1,0:T(8,128)(2,1)S(1)}, bf16[16,512]{1,0:T(8,128)(2,1)S(1)}, u32[]{:S(2)}, u32[]{:S(2)}) collective-permute-start(bf16[16,512]{1,0:T(8,128)(2,1)S(1)} %get-tuple-element.22), channel_id=1, source_target_pairs={{0,1},{1,2},{2,3},{3,0},{4,5},{5,6},{6,7},{7,4},{8,9},{9,10},{10,1... | collective-permute-start | bytes 49160 | tf_op jit(solution)/shard_map/ppermute | solution.py:43
  22.1 6.6 %collective-permute-start.12 = (bf16[16,512]{1,0:T(8,128)(2,1)S(1)}, bf16[16,512]{1,0:T(8,128)(2,1)S(1)}, u32[]{:S(2)}, u32[]{:S(2)}) collective-permute-start(bf16[16,512]{1,0:T(8,128)(2,1)S(1)} %get-tuple-element.23), channel_id=1, source_target_pairs={{0,1},{1,2},{2,3},{3,0},{4,5},{5,6},{6,7},{7,4},{8,9},{9,10},{10,1... | collective-permute-start | bytes 49160 | tf_op jit(solution)/shard_map/ppermute | solution.py:43
  23.8 6.6 %collective-permute-start.21 = (bf16[16,512]{1,0:T(8,128)(2,1)S(1)}, bf16[16,512]{1,0:T(8,128)(2,1)S(1)}, u32[]{:S(2)}, u32[]{:S(2)}) collective-permute-start(bf16[16,512]{1,0:T(8,128)(2,1)S(1)} %get-tuple-element.21), channel_id=1, source_target_pairs={{0,1},{1,2},{2,3},{3,0},{4,5},{5,6},{6,7},{7,4},{8,9},{9,10},{10,1... | collective-permute-start | bytes 49160 | tf_op jit(solution)/shard_map/ppermute | solution.py:43
  25.3 5.5 %collective-permute-start.18 = (bf16[16,512]{1,0:T(8,128)(2,1)S(1)}, bf16[16,512]{1,0:T(8,128)(2,1)S(1)}, u32[]{:S(2)}, u32[]{:S(2)}) collective-permute-start(bf16[16,512]{1,0:T(8,128)(2,1)S(1)} %get-tuple-element.28), channel_id=1, source_target_pairs={{0,1},{1,2},{2,3},{3,0},{4,5},{5,6},{6,7},{7,4},{8,9},{9,10},{10,1... | collective-permute-start | bytes 49160 | tf_op jit(solution)/shard_map/ppermute | solution.py:43
  25.4 6.7 %collective-permute-start.4 = (bf16[16,512]{1,0:T(8,128)(2,1)S(1)}, bf16[16,512]{1,0:T(8,128)(2,1)S(1)}, u32[]{:S(2)}, u32[]{:S(2)}) collective-permute-start(bf16[16,512]{1,0:T(8,128)(2,1)S(1)} %collective-permute-done.3), channel_id=1, source_target_pairs={{0,1},{1,2},{2,3},{3,0},{4,5},{5,6},{6,7},{7,4},{8,9},{9,10},{10,1... | collective-permute-start | bytes 49160 | tf_op jit(solution)/shard_map/ppermute | solution.py:43
  27.1 6.6 %collective-permute-start.1 = (bf16[16,512]{1,0:T(8,128)(2,1)S(1)}, bf16[16,512]{1,0:T(8,128)(2,1)S(1)}, u32[]{:S(2)}, u32[]{:S(2)}) collective-permute-start(bf16[16,512]{1,0:T(8,128)(2,1)S(1)} %collective-permute-done), channel_id=1, source_target_pairs={{0,1},{1,2},{2,3},{3,0},{4,5},{5,6},{6,7},{7,4},{8,9},{9,10},{10,1... | collective-permute-start | bytes 49160 | tf_op jit(solution)/shard_map/ppermute | solution.py:43
  28.7 6.6 %collective-permute-start.10 = (bf16[16,512]{1,0:T(8,128)(2,1)S(1)}, bf16[16,512]{1,0:T(8,128)(2,1)S(1)}, u32[]{:S(2)}, u32[]{:S(2)}) collective-permute-start(bf16[16,512]{1,0:T(8,128)(2,1)S(1)} %collective-permute-done.9), channel_id=1, source_target_pairs={{0,1},{1,2},{2,3},{3,0},{4,5},{5,6},{6,7},{7,4},{8,9},{9,10},{10,1... | collective-permute-start | bytes 49160 | tf_op jit(solution)/shard_map/ppermute | solution.py:43
  30.3 5.5 %collective-permute-start.7 = (bf16[16,512]{1,0:T(8,128)(2,1)S(1)}, bf16[16,512]{1,0:T(8,128)(2,1)S(1)}, u32[]{:S(2)}, u32[]{:S(2)}) collective-permute-start(bf16[16,512]{1,0:T(8,128)(2,1)S(1)} %collective-permute-done.6), channel_id=1, source_target_pairs={{0,1},{1,2},{2,3},{3,0},{4,5},{5,6},{6,7},{7,4},{8,9},{9,10},{10,1... | collective-permute-start | bytes 49160 | tf_op jit(solution)/shard_map/ppermute | solution.py:43
  30.9 6.2 %collective-permute-start.16 = (bf16[16,512]{1,0:T(8,128)(2,1)S(1)}, bf16[16,512]{1,0:T(8,128)(2,1)S(1)}, u32[]{:S(2)}, u32[]{:S(2)}) collective-permute-start(bf16[16,512]{1,0:T(8,128)(2,1)S(1)} %collective-permute-done.15), channel_id=1, source_target_pairs={{0,1},{1,2},{2,3},{3,0},{4,5},{5,6},{6,7},{7,4},{8,9},{9,10},{10,1... | collective-permute-start | bytes 49160 | tf_op jit(solution)/shard_map/ppermute | solution.py:43
  32.1 6.6 %collective-permute-start.13 = (bf16[16,512]{1,0:T(8,128)(2,1)S(1)}, bf16[16,512]{1,0:T(8,128)(2,1)S(1)}, u32[]{:S(2)}, u32[]{:S(2)}) collective-permute-start(bf16[16,512]{1,0:T(8,128)(2,1)S(1)} %collective-permute-done.12), channel_id=1, source_target_pairs={{0,1},{1,2},{2,3},{3,0},{4,5},{5,6},{6,7},{7,4},{8,9},{9,10},{10,1... | collective-permute-start | bytes 49160 | tf_op jit(solution)/shard_map/ppermute | solution.py:43
  33.7 6.6 %collective-permute-start.22 = (bf16[16,512]{1,0:T(8,128)(2,1)S(1)}, bf16[16,512]{1,0:T(8,128)(2,1)S(1)}, u32[]{:S(2)}, u32[]{:S(2)}) collective-permute-start(bf16[16,512]{1,0:T(8,128)(2,1)S(1)} %collective-permute-done.21), channel_id=1, source_target_pairs={{0,1},{1,2},{2,3},{3,0},{4,5},{5,6},{6,7},{7,4},{8,9},{9,10},{10,1... | collective-permute-start | bytes 49160 | tf_op jit(solution)/shard_map/ppermute | solution.py:43
  35.9 6.2 %collective-permute-start.5 = (bf16[16,512]{1,0:T(8,128)(2,1)S(1)}, bf16[16,512]{1,0:T(8,128)(2,1)S(1)}, u32[]{:S(2)}, u32[]{:S(2)}) collective-permute-start(bf16[16,512]{1,0:T(8,128)(2,1)S(1)} %collective-permute-done.4), channel_id=1, source_target_pairs={{0,1},{1,2},{2,3},{3,0},{4,5},{5,6},{6,7},{7,4},{8,9},{9,10},{10,1... | collective-permute-start | bytes 49160 | tf_op jit(solution)/shard_map/ppermute | solution.py:43
  37.1 6.6 %collective-permute-start.2 = (bf16[16,512]{1,0:T(8,128)(2,1)S(1)}, bf16[16,512]{1,0:T(8,128)(2,1)S(1)}, u32[]{:S(2)}, u32[]{:S(2)}) collective-permute-start(bf16[16,512]{1,0:T(8,128)(2,1)S(1)} %collective-permute-done.1), channel_id=1, source_target_pairs={{0,1},{1,2},{2,3},{3,0},{4,5},{5,6},{6,7},{7,4},{8,9},{9,10},{10,1... | collective-permute-start | bytes 49160 | tf_op jit(solution)/shard_map/ppermute | solution.py:43
  38.7 9.6 %collective-permute-start.11 = (bf16[16,512]{1,0:T(8,128)(2,1)S(1)}, bf16[16,512]{1,0:T(8,128)(2,1)S(1)}, u32[]{:S(2)}, u32[]{:S(2)}) collective-permute-start(bf16[16,512]{1,0:T(8,128)(2,1)S(1)} %collective-permute-done.10), channel_id=1, source_target_pairs={{0,1},{1,2},{2,3},{3,0},{4,5},{5,6},{6,7},{7,4},{8,9},{9,10},{10,1... | collective-permute-start | bytes 49160 | tf_op jit(solution)/shard_map/ppermute | solution.py:43
  40.3 9.1 %collective-permute-start.8 = (bf16[16,512]{1,0:T(8,128)(2,1)S(1)}, bf16[16,512]{1,0:T(8,128)(2,1)S(1)}, u32[]{:S(2)}, u32[]{:S(2)}) collective-permute-start(bf16[16,512]{1,0:T(8,128)(2,1)S(1)} %collective-permute-done.7), channel_id=1, source_target_pairs={{0,1},{1,2},{2,3},{3,0},{4,5},{5,6},{6,7},{7,4},{8,9},{9,10},{10,1... | collective-permute-start | bytes 49160 | tf_op jit(solution)/shard_map/ppermute | solution.py:43
  40.8 30.4 %collective-permute-start.17 = (bf16[16,512]{1,0:T(8,128)(2,1)S(1)}, bf16[16,512]{1,0:T(8,128)(2,1)S(1)}, u32[]{:S(2)}, u32[]{:S(2)}) collective-permute-start(bf16[16,512]{1,0:T(8,128)(2,1)S(1)} %collective-permute-done.16), channel_id=1, source_target_pairs={{0,1},{1,2},{2,3},{3,0},{4,5},{5,6},{6,7},{7,4},{8,9},{9,10},{10,1... | collective-permute-start | bytes 49160 | tf_op jit(solution)/shard_map/ppermute | solution.py:43
  42.1 29.2 %collective-permute-start.14 = (bf16[16,512]{1,0:T(8,128)(2,1)S(1)}, bf16[16,512]{1,0:T(8,128)(2,1)S(1)}, u32[]{:S(2)}, u32[]{:S(2)}) collective-permute-start(bf16[16,512]{1,0:T(8,128)(2,1)S(1)} %collective-permute-done.13), channel_id=1, source_target_pairs={{0,1},{1,2},{2,3},{3,0},{4,5},{5,6},{6,7},{7,4},{8,9},{9,10},{10,1... | collective-permute-start | bytes 49160 | tf_op jit(solution)/shard_map/ppermute | solution.py:43
  43.7 38.3 %collective-permute-start.23 = (bf16[16,512]{1,0:T(8,128)(2,1)S(1)}, bf16[16,512]{1,0:T(8,128)(2,1)S(1)}, u32[]{:S(2)}, u32[]{:S(2)}) collective-permute-start(bf16[16,512]{1,0:T(8,128)(2,1)S(1)} %collective-permute-done.22), channel_id=1, source_target_pairs={{0,1},{1,2},{2,3},{3,0},{4,5},{5,6},{6,7},{7,4},{8,9},{9,10},{10,1... | collective-permute-start | bytes 49160 | tf_op jit(solution)/shard_map/ppermute | solution.py:43
  48.4 33.6 %collective-permute-start.20 = (bf16[16,512]{1,0:T(8,128)(2,1)S(1)}, bf16[16,512]{1,0:T(8,128)(2,1)S(1)}, u32[]{:S(2)}, u32[]{:S(2)}) collective-permute-start(bf16[16,512]{1,0:T(8,128)(2,1)S(1)} %collective-permute-done.19), channel_id=1, source_target_pairs={{0,1},{1,2},{2,3},{3,0},{4,5},{5,6},{6,7},{7,4},{8,9},{9,10},{10,1... | collective-permute-start | bytes 49160 | tf_op jit(solution)/shard_map/ppermute | solution.py:43
  (7 other events, 80.5 us)
Sparse Core Ops, SparseCore 0:
  121.3 25.4 reduce-scatter.1
